TPU v7x, 32 devices: a whole 2x2x4 slice. The times are simulated.
32 devices in a mesh: shard: 16 (over z, y, core), model: 2 (over x).
Axes of the slice: x: 2, y: 2, z: 4, core: 2. Of those that a mesh axis runs over, the one named last changes fastest.
Arguments:
- gradients: float32 [128, 128, 4096], P(None, 'shard', 'model'), may hold values from -6 to 6
- momentum: float32 [128, 128, 4096], P(None, 'shard', 'model'), may hold values from -6 to 6
- weights: float32 [128, 128, 4096], P(None, 'shard', 'model'), may hold values from -0.1875 to 0.1875
Outputs:
- new_weights: float32 [128, 128, 4096], P(None, 'shard', 'model')
- new_momentum: float32 [128, 128, 4096], P(None, 'shard', 'model')
All inputs are finite; a program needn't handle non-finite values.
Results may differ from a plain program's by a relative error of at most 0.0001.
Values sent between devices are 32-bit elements; how exact they have to be, the bound alone decides.
No kernel may reach another device: no remote copies, remote signals or barrier semaphores. Data moves between devices by JAX's collectives and lax.ppermute only.
A program may use at most 128 MiB of HBM per device.

v0:
```python
import jax
import jax.numpy as jnp
from jax import lax
from jax.sharding import PartitionSpec as P

ITERS = 3


hold_rate = 0.9
learn_rate = 0.9
decay_rate = 0.1


def body(gradients, momentum, weights):
    new_momentum = hold_rate * momentum + gradients
    moved = lax.all_to_all(new_momentum, "shard", split_axis=0, concat_axis=1, tiled=True)
    total = lax.psum(jnp.sum(moved * moved, axis=(1, 2), keepdims=True), "model")
    iterate = moved * lax.rsqrt(total + 1e-06)
    for step in range(ITERS):
        gram = lax.psum(
            jnp.einsum("mik,mjk->mij", iterate, iterate, precision=lax.Precision.HIGHEST), "model"
        )
        mixed = -4.775 * gram + 2.0315 * jnp.einsum(
            "mij,mjk->mik", gram, gram, precision=lax.Precision.HIGHEST
        )
        iterate = 3.4445 * iterate + jnp.einsum(
            "mij,mjk->mik", mixed, iterate, precision=lax.Precision.HIGHEST
        )
    back = lax.all_to_all(iterate, "shard", split_axis=1, concat_axis=0, tiled=True)
    new_weights = (1.0 - learn_rate * decay_rate) * weights - learn_rate * back
    return (new_weights, new_momentum)


def solution(mesh):
    placed = (P(None, "shard", "model"), P(None, "shard", "model"), P(None, "shard", "model"))
    return jax.shard_map(
        body,
        mesh=mesh,
        in_specs=placed,
        out_specs=(P(None, "shard", "model"), P(None, "shard", "model")),
        check_vma=False,
    )
```

profile of v0, /device:TPU:1, one launch (start us, length us, event | category | flops | bytes accessed | tf_op | source)
XLA Modules:
  0.0 612.6 jit_solution(11765519909520166831)
XLA Ops:
  7.2 12.0 %multiply_add_fusion.3 = f32[128,8,2048]{2,1,0:T(8,128)} fusion(f32[128,8,2048]{2,1,0:T(8,128)} %param.3, f32[128,8,2048]{2,1,0:T(8,128)} %param.4), kind=kLoop, calls=%fused_computation.7 | loop fusion | flops 4194304 | bytes 25165824 | tf_op jit(solution)/shard_map/add | solution.py:15
  19.2 189.9 %all_to_all.27 = f32[128,8,2048]{2,1,0:T(8,128)S(1)} all-to-all(f32[128,8,2048]{2,1,0:T(8,128)} %multiply_add_fusion.3), channel_id=1, replica_groups=mesh['shard'=16,'model'=2] {'shard'}, dimensions={0} | all-to-all | bytes 16777216 | tf_op jit(solution)/shard_map/all_to_all | solution.py:16
  209.1 3.4 copy-done
  212.5 0.8 fusion
  213.3 4.1 psum.28
  217.3 12.9 %fusion.2 = f32[8,128,128]{2,1,0:T(8,128)} fusion(f32[16,8,8,2048]{3,2,1,0:T(8,128)} %bitcast.38, f32[8]{0:T(128)S(1)} %rsqrt_bitcast_fusion), kind=kOutput, calls=%fused_computation.9 | convolution fusion | flops 3223322624 | bytes 8912928 | tf_op jit(solution)/shard_map/mik,mjk->mij/dot_general | solution.py:21
  230.6 29.0 %all-reduce.4.cloned.1.call-done = f32[8,128,128]{2,1,0:T(8,128)} async-done(((f32[8,128,128]{2,1,0:T(8,128)}), f32[8,128,128]{2,1,0:T(8,128)}) %all-reduce.4.cloned.1.call-update) | async-done | bytes 524304 | tf_op jit(solution)/shard_map/psum | solution.py:20
  259.6 2.1 fusion.7
  261.7 12.0 %multiply_add_fusion.2 = f32[8,128,2048]{2,1,0:T(8,128)S(1)} fusion(f32[16,8,8,2048]{3,2,1,0:T(8,128)} %bitcast.39, f32[8,128,128]{2,1,0:T(8,128)S(1)} %fusion.7, f32[8]{0:T(128)S(1)} %rsqrt_bitcast_fusion), kind=kOutput, calls=%fused_computation.6 | convolution fusion | flops 3229614080 | bytes 17301536 | tf_op jit(solution)/shard_map/mij,mjk->mik/dot_general | solution.py:26
  273.7 3.4 copy-done.1
  277.1 8.5 %fusion.8 = f32[8,128,128]{2,1,0:T(8,128)} fusion(f32[8,128,2048]{2,1,0:T(8,128)S(1)} %multiply_add_fusion.2), kind=kOutput, calls=%fused_computation.20 | convolution fusion | flops 3221225472 | bytes 8912896 | tf_op jit(solution)/shard_map/mik,mjk->mij/dot_general | solution.py:21
  285.7 28.8 %all-reduce.6.cloned.1.call-done = f32[8,128,128]{2,1,0:T(8,128)} async-done(((f32[8,128,128]{2,1,0:T(8,128)}), f32[8,128,128]{2,1,0:T(8,128)}) %all-reduce.6.cloned.1.call-update) | async-done | bytes 524304 | tf_op jit(solution)/shard_map/psum | solution.py:20
  314.5 2.1 fusion.6
  316.6 14.1 %multiply_add_fusion.1 = f32[8,128,2048]{2,1,0:T(8,128)S(1)} fusion(f32[8,128,2048]{2,1,0:T(8,128)} %copy-done.1, f32[8,128,128]{2,1,0:T(8,128)S(1)} %fusion.6), kind=kOutput, calls=%fused_computation.5 | convolution fusion | flops 3225419776 | bytes 17301504 | tf_op jit(solution)/shard_map/mij,mjk->mik/dot_general | solution.py:26
  330.7 3.4 copy-done.2
  334.0 8.5 %fusion.9 = f32[8,128,128]{2,1,0:T(8,128)} fusion(f32[8,128,2048]{2,1,0:T(8,128)S(1)} %multiply_add_fusion.1), kind=kOutput, calls=%fused_computation.21 | convolution fusion | flops 3221225472 | bytes 8912896 | tf_op jit(solution)/shard_map/mik,mjk->mij/dot_general | solution.py:21
  342.6 28.8 %all-reduce.8.cloned.1.call-done = f32[8,128,128]{2,1,0:T(8,128)} async-done(((f32[8,128,128]{2,1,0:T(8,128)}), f32[8,128,128]{2,1,0:T(8,128)}) %all-reduce.8.cloned.1.call-update) | async-done | bytes 524304 | tf_op jit(solution)/shard_map/psum | solution.py:20
  371.4 2.1 fusion.5
  373.5 14.8 %multiply_add_fusion = f32[8,128,2048]{2,1,0:T(8,128)S(1)} fusion(f32[8,128,2048]{2,1,0:T(8,128)} %copy-done.2, f32[8,128,128]{2,1,0:T(8,128)S(1)} %fusion.5), kind=kOutput, calls=%fused_computation.4 | convolution fusion | flops 3225419776 | bytes 17301504 | tf_op jit(solution)/shard_map/mij,mjk->mik/dot_general | solution.py:26
  388.3 4.9 copy.8
  393.2 188.9 %all_to_all.28 = f32[8,128,2048]{2,0,1:T(8,128)S(1)} all-to-all(f32[8,128,2048]{2,0,1:T(8,128)S(1)} %copy.8), channel_id=1, replica_groups=mesh['shard'=16,'model'=2] {'shard'}, dimensions={1} | all-to-all | bytes 16777216 | tf_op jit(solution)/shard_map/all_to_all | solution.py:29
  582.1 1.8 broadcast_multiply_fusion
  583.9 9.7 %copy.9 = f32[16,8,8,2048]{3,2,1,0:T(8,128)} copy(f32[16,8,8,2048]{3,1,2,0:T(8,128)S(1)} %bitcast.40) | data formatting | bytes 16777216 | tf_op jit(solution)/shard_map/mul | solution.py:30
  593.6 12.0 %bitcast_subtract_fusion = f32[128,8,2048]{2,1,0:T(8,128)} fusion(f32[16,8,8,2048]{3,2,1,0:T(8,128)} %copy.9, f32[128,8,2048]{2,1,0:T(8,128)} %param.5), kind=kLoop, calls=%fused_computation.1 | loop fusion | flops 4194304 | bytes 25165824 | tf_op jit(solution)/shard_map/sub | solution.py:30
  (10 shorter events, 0.5 us)
Async XLA Ops:
  7.2 252.5 %all-reduce.4.cloned.1.call-start = ((), (), s32[]{:S(2)}) async-start(), calls=%async_computation.2 | async-start | bytes 1048576 | tf_op jit(solution)/shard_map/psum | solution.py:20
  209.1 3.4 copy-start
  230.3 84.2 %all-reduce.6.cloned.1.call-start = ((), (), s32[]{:S(2)}) async-start(), calls=%async_computation.3 | async-start | bytes 1048576 | tf_op jit(solution)/shard_map/psum | solution.py:20
  273.7 3.4 copy-start.1
  285.7 85.7 %all-reduce.8.cloned.1.call-start = ((), (), s32[]{:S(2)}) async-start(), calls=%async_computation.4 | async-start | bytes 1048576 | tf_op jit(solution)/shard_map/psum | solution.py:20
  330.6 3.4 copy-start.2
Sparse Core Ops, SparseCore 0:
  230.4 29.1 all-reduce.3
  285.8 28.6 all-reduce.5
  342.7 28.6 all-reduce.7
where the time goes:
time: 618 us; the launch traced here: 613 us
  blocking collectives  383 us (62%)
  waiting for transfers between devices  86.6 us (14%)
  matrix products  77.1 us (12%)
  other arithmetic  26.6 us (4%)
  local copies, waits for them, and re-layouts  24.7 us (4%)
  between operations  14.3 us (2%)
    all_to_all x1, blocking collectives, body(): lax.all_to_all(new_momentum, 'shard', split_axis=0, concat_axis=1, tiled=...  190 us
    all_to_all x1, blocking collectives, body(): lax.all_to_all(iterate, 'shard', split_axis=1, concat_axis=0, tiled=True)  189 us
    psum x3, waiting for transfers between devices, body(): lax.psum(jnp.einsum('mik,mjk->mij', iterate, iterate, precision=lax.Preci...  86.6 us
    dot_general x3, matrix products, body(): jnp.einsum('mij,mjk->mik', mixed, iterate, precision=lax.Precision.HIGHEST)  40.9 us
    dot_general x3, matrix products, body(): jnp.einsum('mik,mjk->mij', iterate, iterate, precision=lax.Precision.HIGH...  29.9 us
  transfers between devices with their start and end apart: 3, of which 3 were waited for; matrix products, arithmetic and copies ran while one was open for 0% of the time, Pallas kernels for 0%

commit v1 on v0

v1 whole, which is shorter than its diff:
```python
import functools

import jax
import jax.numpy as jnp
from jax import lax
from jax.experimental import pallas as pl
from jax.experimental.pallas import tpu as pltpu
from jax.sharding import PartitionSpec as P

ITERS = 3
CHUNKS = 4

hold_rate = 0.9
learn_rate = 0.9
decay_rate = 0.1


def mm(form, a, b):
    return jnp.einsum(form, a, b, precision=lax.Precision.HIGHEST)


def dot(a, b, contract_b=0):
    return lax.dot_general(
        a, b, (((1,), (contract_b,)), ((), ())),
        precision=lax.Precision.HIGHEST, preferred_element_type=jnp.float32,
    )


def cost(flops, moved):
    return pl.CostEstimate(flops=flops, bytes_accessed=moved, transcendentals=0)


def over_model(part):
    size = lax.axis_size("model")
    total = part
    for hop in range(1, size):
        total = total + lax.ppermute(part, "model", [(i, (i + hop) % size) for i in range(size)])
    return total


def polynomial(raw, product):
    side = raw.shape[-1]
    place = raw.shape[:-2] + (side, side)
    eye = (lax.broadcasted_iota(jnp.int32, place, raw.ndim - 2) == lax.broadcasted_iota(jnp.int32, place, raw.ndim - 1)).astype(jnp.float32)
    total = jnp.sum(jnp.sum(raw * eye, axis=-1, keepdims=True), axis=-2, keepdims=True)
    scale = lax.rsqrt(total + 1e-06)
    gram = (raw * scale) * scale
    chain = None
    for step in range(ITERS):
        poly = 3.4445 * eye - 4.775 * gram + 2.0315 * product(gram, gram)
        chain = poly if chain is None else product(poly, chain)
        if step < ITERS - 1:
            gram = product(poly, product(gram, poly))
    return chain * scale


def momentum_kernel(gradients_ref, momentum_ref, *refs):
    whole_ref, piece_ref = refs[-2:]
    fresh = hold_rate * momentum_ref[...] + gradients_ref[...]
    whole_ref[...] = fresh
    piece_ref[...] = fresh


def momentum_chunk(chunk, gradients, momentum, whole):
    mats, rows, columns = gradients.shape
    count = mats // CHUNKS
    block = min(count, 8)
    first = chunk * count // block
    there = pl.BlockSpec((block, rows, columns), lambda i: (i + first, 0, 0))
    here = pl.BlockSpec((block, rows, columns), lambda i: (i, 0, 0))
    size = count * rows * columns
    return pl.pallas_call(
        momentum_kernel,
        grid=(count // block,),
        in_specs=[there, there] + ([] if whole is None else [pl.BlockSpec(memory_space=pl.ANY)]),
        out_specs=[there, here],
        out_shape=[jax.ShapeDtypeStruct(gradients.shape, jnp.float32), jax.ShapeDtypeStruct((count, rows, columns), jnp.float32)],
        input_output_aliases={} if whole is None else {2: 0},
        cost_estimate=cost(2 * size, 16 * size),
        name="momentum",
    )(gradients, momentum, *([] if whole is None else [whole]))


def weights_kernel(weights_ref, back_ref, *refs):
    refs[-1][...] = (1.0 - learn_rate * decay_rate) * weights_ref[...] - learn_rate * back_ref[...]


def weights_chunk(chunk, weights, back, whole):
    mats, rows, columns = weights.shape
    count = mats // CHUNKS
    block = min(count, 8)
    first = chunk * count // block
    there = pl.BlockSpec((block, rows, columns), lambda i: (i + first, 0, 0))
    here = pl.BlockSpec((block, rows, columns), lambda i: (i, 0, 0))
    size = count * rows * columns
    return pl.pallas_call(
        weights_kernel,
        grid=(count // block,),
        in_specs=[there, here] + ([] if whole is None else [pl.BlockSpec(memory_space=pl.ANY)]),
        out_specs=there,
        out_shape=jax.ShapeDtypeStruct(weights.shape, jnp.float32),
        input_output_aliases={} if whole is None else {2: 0},
        cost_estimate=cost(3 * size, 12 * size),
        name="weights",
    )(weights, back, *([] if whole is None else [whole]))


def gram_kernel(stack_ref, out_ref):
    owners, _, rows, columns = stack_ref.shape
    stack = stack_ref[...].reshape(owners * rows, columns)
    out_ref[0] = dot(stack, stack, 1)


def gram_of(arrived):
    owners, mats, rows, columns = arrived.shape
    side = owners * rows
    return pl.pallas_call(
        gram_kernel,
        grid=(mats,),
        in_specs=[pl.BlockSpec((owners, 1, rows, columns), lambda i: (0, i, 0, 0))],
        out_specs=pl.BlockSpec((1, side, side), lambda i: (i, 0, 0)),
        out_shape=jax.ShapeDtypeStruct((mats, side, side), jnp.float32),
        cost_estimate=cost(12 * mats * side * side * columns, 4 * mats * side * columns),
        name="gram",
    )(arrived)


def apply_kernel(gram_ref, stack_ref, out_ref):
    owners, _, rows, columns = stack_ref.shape
    chain = polynomial(gram_ref[0], dot)
    stack = stack_ref[...].reshape(owners * rows, columns)
    out_ref[...] = dot(chain, stack).reshape(owners, 1, rows, columns)


def apply_of(gram, arrived):
    owners, mats, rows, columns = arrived.shape
    side = owners * rows
    spot = pl.BlockSpec((owners, 1, rows, columns), lambda i: (0, i, 0, 0))
    return pl.pallas_call(
        apply_kernel,
        grid=(mats,),
        in_specs=[pl.BlockSpec((1, side, side), lambda i: (i, 0, 0)), spot],
        out_specs=spot,
        out_shape=jax.ShapeDtypeStruct(arrived.shape, jnp.float32),
        cost_estimate=cost(12 * mats * side * side * (columns + 9 * side), 8 * mats * side * columns),
        name="apply",
    )(gram, arrived)


def exchange(piece):
    return lax.all_to_all(piece, "shard", split_axis=0, concat_axis=0, tiled=True)


def body(gradients, momentum, weights):
    owners = lax.axis_size("shard")
    mats, rows, columns = gradients.shape
    held = mats // (CHUNKS * owners)
    whole, arrived = None, []
    for c in range(CHUNKS):
        whole, piece = momentum_chunk(c, gradients, momentum, whole)
        arrived.append(exchange(piece.reshape(owners, held, rows, columns)))
    updated = None
    for c in range(CHUNKS):
        gram = over_model(gram_of(arrived[c]))
        back = exchange(apply_of(gram, arrived[c]))
        updated = weights_chunk(c, weights, back.reshape(owners * held, rows, columns), updated)
    return (updated, whole)


def small_body(gradients, momentum, weights):
    new_momentum = hold_rate * momentum + gradients
    stack = lax.all_to_all(new_momentum, "shard", split_axis=0, concat_axis=1, tiled=True)
    gram = over_model(mm("mik,mjk->mij", stack, stack))
    chain = polynomial(gram, functools.partial(mm, "mij,mjk->mik"))
    back = lax.all_to_all(mm("mij,mjk->mik", chain, stack), "shard", split_axis=1, concat_axis=0, tiled=True)
    return ((1.0 - learn_rate * decay_rate) * weights - learn_rate * back, new_momentum)


def pick(gradients, momentum, weights):
    mats, rows, columns = gradients.shape
    fits = rows % 8 == 0 and columns % 128 == 0 and mats % (CHUNKS * lax.axis_size("shard")) == 0
    return (body if fits else small_body)(gradients, momentum, weights)


def solution(mesh):
    placed = P(None, "shard", "model")
    return jax.shard_map(pick, mesh=mesh, in_specs=(placed,) * 3, out_specs=(placed,) * 2, check_vma=False)
```

time: 618 us -> 443 us (0.72)
  blocking collectives: 383 us -> 55.1 us
  waiting for transfers between devices: 86.6 us -> 210 us
  Pallas kernels: 0 us -> 83.2 us
  matrix products: 77.1 us -> 0 us
  starting transfers between devices: 0.41 us -> 73.4 us
  other arithmetic: 26.6 us -> 6.3 us
  local copies, waits for them, and re-layouts: 24.7 us -> 7.96 us
  between operations: 14.3 us -> 0.66 us
    all_to_all x2 -> x1, blocking collectives: 379 us -> 55.1 us  [exchange(): lax.all_to_all(piece, 'shard', split_axis=0, concat_axis=0, tiled=True)]
    all_to_all x0 -> x7, waiting for transfers between devices: none -> 194 us  [exchange(): lax.all_to_all(piece, 'shard', split_axis=0, concat_axis=0, tiled=True)]
    psum x3 -> x0, waiting for transfers between devices: 86.6 us -> none  [body(): lax.psum(jnp.einsum('mik,mjk->mij', iterate, iterate, precision=lax.Preci...]
    pallas_call x0 -> x16, Pallas kernels: none -> 83.2 us  [the longest x4 31.9 us: apply_of(): pl.pallas_call(apply_kernel, grid=(mats,), in_specs=[pl.BlockSpec((1, sid...]
    dot_general x9 -> x0, matrix products: 77.1 us -> none  [the longest x3 40.9 us: body(): jnp.einsum('mij,mjk->mik', mixed, iterate, precision=lax.Precision.HIGHEST)]
    all_to_all x0 -> x7, starting transfers between devices: none -> 68.6 us  [exchange(): lax.all_to_all(piece, 'shard', split_axis=0, concat_axis=0, tiled=True)]
    ppermute x0 -> x4, waiting for transfers between devices: none -> 15.8 us  [over_model(): lax.ppermute(part, 'model', [(i, (i + hop) % size) for i in range(size)])]
    sub x1 -> x0, other arithmetic: 12 us -> none  [body(): new_weights = (1.0 - learn_rate * decay_rate) * weights - learn_rate * back]
  transfers between devices with their start and end apart: 3 -> 11, of which waited for: 3 -> 11; matrix products, arithmetic and copies ran while one was open for 0% -> 1% of each run, Pallas kernels for 0% -> 16%
where the time goes in v1:
time: 443 us; the launch traced here: 437 us
  waiting for transfers between devices  210 us (47%)
  Pallas kernels  83.2 us (19%)
  starting transfers between devices  73.4 us (17%)
  blocking collectives  55.1 us (12%)
  local copies, waits for them, and re-layouts  7.96 us (2%)
  other arithmetic  6.3 us (1%)
    all_to_all x7, waiting for transfers between devices, exchange(): lax.all_to_all(piece, 'shard', split_axis=0, concat_axis=0, tiled=True)  194 us
    all_to_all x7, starting transfers between devices, exchange(): lax.all_to_all(piece, 'shard', split_axis=0, concat_axis=0, tiled=True)  68.6 us
    all_to_all x1, blocking collectives, exchange(): lax.all_to_all(piece, 'shard', split_axis=0, concat_axis=0, tiled=True)  55.1 us
    pallas_call x4, Pallas kernels, apply_of(): pl.pallas_call(apply_kernel, grid=(mats,), in_specs=[pl.BlockSpec((1, sid...  31.9 us
    pallas_call x4, Pallas kernels, momentum_chunk(): pl.pallas_call(momentum_kernel, grid=(count // block,), in_specs=[there,...  18.8 us
    pallas_call x4, Pallas kernels, weights_chunk(): pl.pallas_call(weights_kernel, grid=(count // block,), in_specs=[there, h...  16.9 us
    ppermute x4, waiting for transfers between devices, over_model(): lax.ppermute(part, 'model', [(i, (i + hop) % size) for i in range(size)])  15.8 us
    pallas_call x4, Pallas kernels, gram_of(): pl.pallas_call(gram_kernel, grid=(mats,), in_specs=[pl.BlockSpec((owners,...  15.6 us
  transfers between devices with their start and end apart: 11, of which 11 were waited for; matrix products, arithmetic and copies ran while one was open for 1% of the time, Pallas kernels for 16%

profile of v1, /device:TPU:1, one launch (start us, length us, event | category | flops | bytes accessed | tf_op | source)
XLA Modules:
  0.0 436.8 jit_solution(9981619744418844798)
XLA Ops:
  0.6 4.7 %momentum.4 = (f32[128,8,2048]{2,1,0:T(8,128)}, f32[32,8,2048]{2,1,0:T(8,128)}) custom-call(f32[128,8,2048]{2,1,0:T(8,128)} %gradients_ref.7, f32[128,8,2048]{2,1,0:T(8,128)} %momentum_ref.7), custom_call_target="tpu_custom_call" | custom-call | flops 1048576 | bytes 8388608 | tf_op jit(solution)/shard_map/momentum/pallas_call | solution.py:72
  5.3 4.7 %momentum.5 = (f32[128,8,2048]{2,1,0:T(8,128)}, f32[32,8,2048]{2,1,0:T(8,128)}) custom-call(f32[128,8,2048]{2,1,0:T(8,128)} %gradients_ref.7, f32[128,8,2048]{2,1,0:T(8,128)} %momentum_ref.7, f32[128,8,2048]{2,1,0:T(8,128)} %get-tuple-element.10.refs_0_), custom_call_target="tpu_custom_call", output_to_operand_aliasing={{0}: (2, {})} | custom-call | flops 1048576 | bytes 8388608 | tf_op jit(solution)/shard_map/momentum/pallas_call | solution.py:72
  10.0 55.1 %all_to_all.40.stack_ref = f32[16,2,8,2048]{3,2,1,0:T(8,128)} all-to-all(f32[16,2,8,2048]{3,2,1,0:T(8,128)} %bitcast.14), channel_id=1, replica_groups=mesh['shard'=16,'model'=2] {'shard'}, dimensions={0} | all-to-all | bytes 4194304 | tf_op jit(solution)/shard_map/all_to_all | solution.py:151
  65.2 4.6 %all-to-all-start.6 = ((f32[16,2,8,2048]{3,2,1,0:T(8,128)}), f32[16,2,8,2048]{3,2,1,0:T(8,128)S(1)}, u32[]{:S(2)}, u32[]{:S(2)}) async-start(f32[16,2,8,2048]{3,2,1,0:T(8,128)} %bitcast.12), calls=%async_computation.6 | async-start | bytes 4194304 | tf_op jit(solution)/shard_map/all_to_all | solution.py:151
  69.7 4.7 %momentum.6 = (f32[128,8,2048]{2,1,0:T(8,128)}, f32[32,8,2048]{2,1,0:T(8,128)}) custom-call(f32[128,8,2048]{2,1,0:T(8,128)} %gradients_ref.7, f32[128,8,2048]{2,1,0:T(8,128)} %momentum_ref.7, f32[128,8,2048]{2,1,0:T(8,128)} %get-tuple-element.11.refs_0_), custom_call_target="tpu_custom_call", output_to_operand_aliasing={{0}: (2, {})} | custom-call | flops 1048576 | bytes 8388608 | tf_op jit(solution)/shard_map/momentum/pallas_call | solution.py:72
  74.4 36.8 %all-to-all-done.6.stack_ref = f32[16,2,8,2048]{3,2,1,0:T(8,128)S(1)} async-done(((f32[16,2,8,2048]{3,2,1,0:T(8,128)}), f32[16,2,8,2048]{3,2,1,0:T(8,128)S(1)}, u32[]{:S(2)}, u32[]{:S(2)}) %all-to-all-start.6) | async-done | bytes 2097184 | tf_op jit(solution)/shard_map/all_to_all | solution.py:151
  112.6 10.7 %all-to-all-start.2 = ((f32[16,2,8,2048]{3,2,1,0:T(8,128)}), f32[16,2,8,2048]{3,2,1,0:T(8,128)S(1)}, u32[]{:S(2)}, u32[]{:S(2)}) async-start(f32[16,2,8,2048]{3,2,1,0:T(8,128)} %bitcast.13), calls=%async_computation.2 | async-start | bytes 4194304 | tf_op jit(solution)/shard_map/all_to_all | solution.py:151
  123.2 4.7 %momentum.7 = (f32[128,8,2048]{2,1,0:T(8,128)}, f32[32,8,2048]{2,1,0:T(8,128)}) custom-call(f32[128,8,2048]{2,1,0:T(8,128)} %gradients_ref.7, f32[128,8,2048]{2,1,0:T(8,128)} %momentum_ref.7, f32[128,8,2048]{2,1,0:T(8,128)} %get-tuple-element.12.refs_0_), custom_call_target="tpu_custom_call", output_to_operand_aliasing={{0}: (2, {})} | custom-call | flops 1048576 | bytes 8388608 | tf_op jit(solution)/shard_map/momentum/pallas_call | solution.py:72
  127.9 36.8 %all-to-all-done.2.stack_ref = f32[16,2,8,2048]{3,2,1,0:T(8,128)S(1)} async-done(((f32[16,2,8,2048]{3,2,1,0:T(8,128)}), f32[16,2,8,2048]{3,2,1,0:T(8,128)S(1)}, u32[]{:S(2)}, u32[]{:S(2)}) %all-to-all-start.2) | async-done | bytes 2097184 | tf_op jit(solution)/shard_map/all_to_all | solution.py:151
  166.1 10.7 %all-to-all-start = ((f32[16,2,8,2048]{3,2,1,0:T(8,128)}), f32[16,2,8,2048]{3,2,1,0:T(8,128)S(1)}, u32[]{:S(2)}, u32[]{:S(2)}) async-start(f32[16,2,8,2048]{3,2,1,0:T(8,128)} %bitcast.11), calls=%async_computation | async-start | bytes 4194304 | tf_op jit(solution)/shard_map/all_to_all | solution.py:151
  187.4 8.0 %apply.6 = f32[16,2,8,2048]{3,2,1,0:T(8,128)} custom-call(f32[2,128,128]{2,1,0:T(8,128)} %add.14.gram_ref, f32[16,2,8,2048]{3,2,1,0:T(8,128)} %all_to_all.40.stack_ref), custom_call_target="tpu_custom_call" | custom-call | flops 1258291200 | bytes 4194304 | tf_op jit(solution)/shard_map/apply/pallas_call | solution.py:139
  195.4 22.9 %all-to-all-done.stack_ref = f32[16,2,8,2048]{3,2,1,0:T(8,128)S(1)} async-done(((f32[16,2,8,2048]{3,2,1,0:T(8,128)}), f32[16,2,8,2048]{3,2,1,0:T(8,128)S(1)}, u32[]{:S(2)}, u32[]{:S(2)}) %all-to-all-start) | async-done | bytes 2097184 | tf_op jit(solution)/shard_map/all_to_all | solution.py:151
  219.6 10.7 %all-to-all-start.5 = ((f32[16,2,8,2048]{3,2,1,0:T(8,128)}), f32[16,2,8,2048]{3,2,1,0:T(8,128)S(1)}, u32[]{:S(2)}, u32[]{:S(2)}) async-start(f32[16,2,8,2048]{3,2,1,0:T(8,128)} %apply.6), calls=%async_computation.5 | async-start | bytes 4194304 | tf_op jit(solution)/shard_map/all_to_all | solution.py:151
  240.9 8.0 %apply.7 = f32[16,2,8,2048]{3,2,1,0:T(8,128)} custom-call(f32[2,128,128]{2,1,0:T(8,128)} %add.15.gram_ref, f32[16,2,8,2048]{3,2,1,0:T(8,128)} %copy-done.5), custom_call_target="tpu_custom_call" | custom-call | flops 1258291200 | bytes 4194304 | tf_op jit(solution)/shard_map/apply/pallas_call | solution.py:139
  248.9 22.9 %all-to-all-done.5 = f32[16,2,8,2048]{3,2,1,0:T(8,128)S(1)} async-done(((f32[16,2,8,2048]{3,2,1,0:T(8,128)}), f32[16,2,8,2048]{3,2,1,0:T(8,128)S(1)}, u32[]{:S(2)}, u32[]{:S(2)}) %all-to-all-start.5) | async-done | bytes 2097184 | tf_op jit(solution)/shard_map/all_to_all | solution.py:151
  273.1 10.7 %all-to-all-start.7 = ((f32[16,2,8,2048]{3,2,1,0:T(8,128)}), f32[16,2,8,2048]{3,2,1,0:T(8,128)S(1)}, u32[]{:S(2)}, u32[]{:S(2)}) async-start(f32[16,2,8,2048]{3,2,1,0:T(8,128)} %apply.7), calls=%async_computation.7 | async-start | bytes 4194304 | tf_op jit(solution)/shard_map/all_to_all | solution.py:151
  294.4 8.0 %apply.5 = f32[16,2,8,2048]{3,2,1,0:T(8,128)} custom-call(f32[2,128,128]{2,1,0:T(8,128)} %add.13.gram_ref, f32[16,2,8,2048]{3,2,1,0:T(8,128)} %copy-done.4), custom_call_target="tpu_custom_call" | custom-call | flops 1258291200 | bytes 4194304 | tf_op jit(solution)/shard_map/apply/pallas_call | solution.py:139
  302.4 22.9 %all-to-all-done.7 = f32[16,2,8,2048]{3,2,1,0:T(8,128)S(1)} async-done(((f32[16,2,8,2048]{3,2,1,0:T(8,128)}), f32[16,2,8,2048]{3,2,1,0:T(8,128)S(1)}, u32[]{:S(2)}, u32[]{:S(2)}) %all-to-all-start.7) | async-done | bytes 2097184 | tf_op jit(solution)/shard_map/all_to_all | solution.py:151
  326.7 10.7 %all-to-all-start.3 = ((f32[16,2,8,2048]{3,2,1,0:T(8,128)}), f32[16,2,8,2048]{3,2,1,0:T(8,128)}, u32[]{:S(2)}, u32[]{:S(2)}) async-start(f32[16,2,8,2048]{3,2,1,0:T(8,128)} %apply.5), calls=%async_computation.3 | async-start | bytes 4194304 | tf_op jit(solution)/shard_map/all_to_all | solution.py:151
  348.0 8.0 %apply.4 = f32[16,2,8,2048]{3,2,1,0:T(8,128)} custom-call(f32[2,128,128]{2,1,0:T(8,128)} %add.12.gram_ref, f32[16,2,8,2048]{3,2,1,0:T(8,128)} %copy-done.3), custom_call_target="tpu_custom_call" | custom-call | flops 1258291200 | bytes 4194304 | tf_op jit(solution)/shard_map/apply/pallas_call | solution.py:139
  356.0 23.0 %all-to-all-done.3 = f32[16,2,8,2048]{3,2,1,0:T(8,128)} async-done(((f32[16,2,8,2048]{3,2,1,0:T(8,128)}), f32[16,2,8,2048]{3,2,1,0:T(8,128)}, u32[]{:S(2)}, u32[]{:S(2)}) %all-to-all-start.3) | async-done | bytes 2097184 | tf_op jit(solution)/shard_map/all_to_all | solution.py:151
  379.0 10.7 %all-to-all-start.1 = ((f32[16,2,8,2048]{3,2,1,0:T(8,128)}), f32[16,2,8,2048]{3,2,1,0:T(8,128)S(1)}, u32[]{:S(2)}, u32[]{:S(2)}) async-start(f32[16,2,8,2048]{3,2,1,0:T(8,128)} %apply.4), calls=%async_computation.1 | async-start | bytes 4194304 | tf_op jit(solution)/shard_map/all_to_all | solution.py:151
  389.7 4.2 weights.4.refs_0_
  402.4 28.8 %all-to-all-done.1 = f32[16,2,8,2048]{3,2,1,0:T(8,128)S(1)} async-done(((f32[16,2,8,2048]{3,2,1,0:T(8,128)}), f32[16,2,8,2048]{3,2,1,0:T(8,128)S(1)}, u32[]{:S(2)}, u32[]{:S(2)}) %all-to-all-start.1) | async-done | bytes 2097184 | tf_op jit(solution)/shard_map/all_to_all | solution.py:151
  (31 shorter events, 63.3 us)
Async XLA Ops:
  65.2 46.1 %all-to-all-start.6 = ((f32[16,2,8,2048]{3,2,1,0:T(8,128)}), f32[16,2,8,2048]{3,2,1,0:T(8,128)S(1)}, u32[]{:S(2)}, u32[]{:S(2)}) async-start(f32[16,2,8,2048]{3,2,1,0:T(8,128)} %bitcast.12), calls=%async_computation.6 | async-start | bytes 4194304 | tf_op jit(solution)/shard_map/all_to_all | solution.py:151
  111.3 1.3 copy-start.5
  112.6 52.2 %all-to-all-start.2 = ((f32[16,2,8,2048]{3,2,1,0:T(8,128)}), f32[16,2,8,2048]{3,2,1,0:T(8,128)S(1)}, u32[]{:S(2)}, u32[]{:S(2)}) async-start(f32[16,2,8,2048]{3,2,1,0:T(8,128)} %bitcast.13), calls=%async_computation.2 | async-start | bytes 4194304 | tf_op jit(solution)/shard_map/all_to_all | solution.py:151
  164.8 1.3 copy-start.4
  166.1 52.2 %all-to-all-start = ((f32[16,2,8,2048]{3,2,1,0:T(8,128)}), f32[16,2,8,2048]{3,2,1,0:T(8,128)S(1)}, u32[]{:S(2)}, u32[]{:S(2)}) async-start(f32[16,2,8,2048]{3,2,1,0:T(8,128)} %bitcast.11), calls=%async_computation | async-start | bytes 4194304 | tf_op jit(solution)/shard_map/all_to_all | solution.py:151
  180.7 5.2 %collective-permute-start.2 = (f32[2,128,128]{2,1,0:T(8,128)}, f32[2,128,128]{2,1,0:T(8,128)S(1)}, u32[]{:S(2)}, u32[]{:S(2)}) collective-permute-start(f32[2,128,128]{2,1,0:T(8,128)} %gram.6), channel_id=1, source_target_pairs={{0,1},{1,0},{2,3},{3,2},{4,5},{5,4},{6,7},{7,6},{8,9},{9,8},{10,11... | collective-permute-start | bytes 393224 | tf_op jit(solution)/shard_map/ppermute | solution.py:37
  218.3 1.3 copy-start.3
  219.6 52.2 %all-to-all-start.5 = ((f32[16,2,8,2048]{3,2,1,0:T(8,128)}), f32[16,2,8,2048]{3,2,1,0:T(8,128)S(1)}, u32[]{:S(2)}, u32[]{:S(2)}) async-start(f32[16,2,8,2048]{3,2,1,0:T(8,128)} %apply.6), calls=%async_computation.5 | async-start | bytes 4194304 | tf_op jit(solution)/shard_map/all_to_all | solution.py:151
  234.2 5.2 %collective-permute-start.3 = (f32[2,128,128]{2,1,0:T(8,128)}, f32[2,128,128]{2,1,0:T(8,128)S(1)}, u32[]{:S(2)}, u32[]{:S(2)}) collective-permute-start(f32[2,128,128]{2,1,0:T(8,128)} %gram.7), channel_id=1, source_target_pairs={{0,1},{1,0},{2,3},{3,2},{4,5},{5,4},{6,7},{7,6},{8,9},{9,8},{10,11... | collective-permute-start | bytes 393224 | tf_op jit(solution)/shard_map/ppermute | solution.py:37
  271.8 1.3 copy-start.1
  273.1 52.2 %all-to-all-start.7 = ((f32[16,2,8,2048]{3,2,1,0:T(8,128)}), f32[16,2,8,2048]{3,2,1,0:T(8,128)S(1)}, u32[]{:S(2)}, u32[]{:S(2)}) async-start(f32[16,2,8,2048]{3,2,1,0:T(8,128)} %apply.7), calls=%async_computation.7 | async-start | bytes 4194304 | tf_op jit(solution)/shard_map/all_to_all | solution.py:151
  287.7 5.2 %collective-permute-start.1 = (f32[2,128,128]{2,1,0:T(8,128)}, f32[2,128,128]{2,1,0:T(8,128)S(1)}, u32[]{:S(2)}, u32[]{:S(2)}) collective-permute-start(f32[2,128,128]{2,1,0:T(8,128)} %gram.5), channel_id=1, source_target_pairs={{0,1},{1,0},{2,3},{3,2},{4,5},{5,4},{6,7},{7,6},{8,9},{9,8},{10,11... | collective-permute-start | bytes 393224 | tf_op jit(solution)/shard_map/ppermute | solution.py:37
  325.3 1.4 copy-start
  326.7 52.3 %all-to-all-start.3 = ((f32[16,2,8,2048]{3,2,1,0:T(8,128)}), f32[16,2,8,2048]{3,2,1,0:T(8,128)}, u32[]{:S(2)}, u32[]{:S(2)}) async-start(f32[16,2,8,2048]{3,2,1,0:T(8,128)} %apply.5), calls=%async_computation.3 | async-start | bytes 4194304 | tf_op jit(solution)/shard_map/all_to_all | solution.py:151
  341.3 5.2 %collective-permute-start = (f32[2,128,128]{2,1,0:T(8,128)}, f32[2,128,128]{2,1,0:T(8,128)S(1)}, u32[]{:S(2)}, u32[]{:S(2)}) collective-permute-start(f32[2,128,128]{2,1,0:T(8,128)} %gram.4), channel_id=1, source_target_pairs={{0,1},{1,0},{2,3},{3,2},{4,5},{5,4},{6,7},{7,6},{8,9},{9,8},{10,11... | collective-permute-start | bytes 393224 | tf_op jit(solution)/shard_map/ppermute | solution.py:37
  379.0 52.2 %all-to-all-start.1 = ((f32[16,2,8,2048]{3,2,1,0:T(8,128)}), f32[16,2,8,2048]{3,2,1,0:T(8,128)S(1)}, u32[]{:S(2)}, u32[]{:S(2)}) async-start(f32[16,2,8,2048]{3,2,1,0:T(8,128)} %apply.4), calls=%async_computation.1 | async-start | bytes 4194304 | tf_op jit(solution)/shard_map/all_to_all | solution.py:151
  431.2 1.3 copy-start.2
